TPU v7x, 32 devices: a whole 2x2x4 slice. The times are simulated.
32 devices in a mesh: dp: 4 (over x, core), mp: 8 (over z, y).
Axes of the slice: x: 2, y: 2, z: 4, core: 2. Of those that a mesh axis runs over, the one named last changes fastest.
Arguments:
- cotangent: bfloat16 [512, 4608], P(('dp', 'mp')), may hold values from -50 to 50
- mlp_out: bfloat16 [512, 4608], P(('dp', 'mp')), may hold values from -500 to 500
- post_gain: float32 [4608], replicated, may hold values from 0.5 to 1.5
- down_weight: bfloat16 [36864, 4608], P('mp', 'dp'), may hold values from -0.09375 to 0.09375
- gate_pre: bfloat16 [512, 36864], P('dp', 'mp'), may hold values from -6 to 6
- up_pre: bfloat16 [512, 36864], P('dp', 'mp'), may hold values from -6 to 6
Outputs:
- gate_grad: float32 [512, 36864], P('dp', 'mp')
- up_grad: float32 [512, 36864], P('dp', 'mp')
- gain_grad: float32 [4608], replicated
All inputs are finite; a program needn't handle non-finite values.
Results may differ from a plain program's by a relative error of at most 0.0005.
Values may be sent and summed in bfloat16 or wider, within the bound.
A program may use at most 64 MiB of HBM per device.

v0:
```python
import functools
import math

import jax
import jax.numpy as jnp
from jax import lax
from jax.experimental import pallas as pl
from jax.experimental.pallas import tpu as pltpu
from jax.sharding import PartitionSpec as P

MESH = pl.DeviceIdType.MESH
LANES = 128
WEIGHT_MAX = 0.09375

epsilon = 1e-06


def gelu_tanh(values):
    return jax.nn.gelu(values, approximate=True)


def encode(values, gain):
    v = values * gain
    v2 = v * v
    v4 = v2 * v2
    v8 = v4 * v4
    return jnp.where(v < 0, -v8, v8).astype(jnp.bfloat16)


def decode(codes, gain):
    b = codes.astype(jnp.float32)
    size = jnp.abs(b)
    root = jnp.exp(jnp.log(size) * 0.125) * (1.0 / gain)
    root = jnp.where(size > 0, root, 0.0)
    return jnp.where(b < 0, -root, root)


def kernel(
    dp, mp, gain, tile,
    c_ref, y_ref, post_ref, w_hbm, out_ref, gain_out,
    w_ref, grad, code, lhs, part, other, sent, got, gsum, gsend_a, grecv_a, grecv_b, gblock,
    w_sem, a_send, a_recv, ga_send, ga_recv, g_recv, z_send, y_send, gb_send, gb_recv,
    d_send, d_recv, x_send, x_recv, go_send, go_recv,
):
    d, m = lax.axis_index("dp"), lax.axis_index("mp")
    nx, nz = dp // 2, mp // 2
    x, core = d // 2, lax.rem(d, 2)
    z, y = m // 2, lax.rem(m, 2)
    rows, full = c_ref.shape
    feat = full // dp
    half = w_ref.shape[0] // 2

    def remote(src, dst, send, recv, dev):
        return pltpu.make_async_remote_copy(
            src_ref=src, dst_ref=dst, send_sem=send, recv_sem=recv, device_id=dev, device_id_type=MESH
        )

    w_copy = pltpu.make_async_copy(w_hbm, w_ref, w_sem)
    w_copy.start()

    barrier = pltpu.get_barrier_semaphore()
    for j in range(1, dp):
        pl.semaphore_signal(barrier, inc=1, device_id=(lax.rem(d + j, dp), m), device_id_type=MESH)
    for j in range(1, mp):
        pl.semaphore_signal(barrier, inc=1, device_id=(d, lax.rem(m + j, mp)), device_id_type=MESH)

    forward = y_ref[...].astype(jnp.float32)
    upstream = c_ref[...].astype(jnp.float32)
    inv = 1.0 / jnp.sqrt(jnp.mean(forward * forward, axis=1, keepdims=True) + epsilon)
    normed = forward * inv
    gain_part = jnp.sum(upstream * normed, axis=0, keepdims=True)
    scaled = upstream * post_ref[...]
    mean_prod = jnp.sum(scaled * normed, axis=1, keepdims=True) * (1.0 / full)
    out_grad = (scaled - normed * mean_prod) * inv
    top = jnp.max(jnp.abs(out_grad), axis=1, keepdims=True).astype(jnp.bfloat16).astype(jnp.float32)
    top = jnp.where(top > 1e-37, top, 1.0)
    codes = encode(out_grad * (1.0 / top), gain)
    top_wide = jnp.broadcast_to(top, (rows, LANES)).astype(jnp.bfloat16)
    for t in range(dp):
        code[t, :, :feat] = codes[:, t * feat:(t + 1) * feat]
        code[t, :, feat:] = top_wide
        gsend_a[t] = gain_part[:, t * feat:(t + 1) * feat]
    grad[m, d] = code[d]

    pl.semaphore_wait(barrier, dp - 1 + mp - 1)

    def a_copy(j):
        t = lax.rem(d + j, dp)
        return remote(code.at[t], grad.at[m, d], a_send.at[j], a_recv.at[j], (t, m))

    def ga_copy(j):
        t = lax.rem(d + j, dp)
        return remote(gsend_a.at[t], grecv_a.at[j], ga_send.at[j], ga_recv.at[j], (t, m))

    for j in range(1, dp):
        a_copy(j).start()
    for j in range(1, dp):
        ga_copy(j).start()
    for j in range(1, dp):
        a_copy(j).wait_recv()

    def chunk_z(p):
        odd = lax.rem(p, 2)
        off = odd * ((p + 1) // 2) - (1 - odd) * (p // 2)
        return lax.rem(z + off + nz, nz)

    def chunk(k):
        q = lax.rem(k, 2)
        return 2 * chunk_z(k // 2) + lax.rem(y + q, 2)

    def z_copy(p):
        return remote(grad.at[m], grad.at[m], z_send.at[p], g_recv.at[m], (d, 2 * chunk_z(p) + y))

    def y_copy(p):
        mine = 2 * chunk_z(p) + y
        return remote(grad.at[mine], grad.at[mine], y_send.at[p], g_recv.at[mine], (d, 2 * z + 1 - y))

    def g_wait(mc):
        remote(grad.at[mc], grad.at[mc], y_send.at[0], g_recv.at[mc], (d, 2 * z + 1 - y)).wait_recv()

    y_copy(0).start()
    for p in range(1, nz):
        z_copy(p).start()

    for j in range(1, dp):
        ga_copy(j).wait_recv()
    total = gsend_a[d]
    for j in range(1, dp):
        total = total + grecv_a[j]
    gsum[...] = total

    def gb_copy(j):
        return remote(gsum, grecv_b.at[j], gb_send.at[j], gb_recv.at[j], (d, lax.rem(m + j, mp)))

    for j in range(1, mp):
        gb_copy(j).start()

    w_copy.wait()

    def d_copy(k, xo):
        return remote(
            part.at[k, 2 * xo + 1 - core], other.at[k, xo], d_send.at[k, xo], d_recv.at[k, xo], (2 * x + 1 - core, m)
        )

    def x_copy(k, j):
        return remote(
            sent.at[k, j - 1], got.at[k, j - 1], x_send.at[k, j - 1], x_recv.at[k, j - 1],
            (2 * lax.rem(x + j, nx) + core, m),
        )

    def unpack(p):
        for q in range(2):
            mc = chunk(2 * p + q)
            for t in range(dp):
                value = decode(grad[mc, t][:, :feat], gain)
                high = value.astype(jnp.bfloat16)
                at = (2 * t + q) * rows
                lhs[at:at + rows, :] = high
                lhs[2 * dp * rows + at:2 * dp * rows + at + rows, :] = (
                    value - high.astype(jnp.float32)
                ).astype(jnp.bfloat16)

    def compute(k):
        first = lax.rem(k, 2) * half

        def one(i, carry):
            units = pl.ds(pl.multiple_of(first + i * tile, tile), tile)
            cols = pl.ds(pl.multiple_of(i * tile, tile), tile)
            both = lax.dot_general(
                lhs[...], w_ref[units, :], (((1,), (1,)), ((), ())), preferred_element_type=jnp.float32
            )
            both = both[: 2 * dp * rows] + both[2 * dp * rows:]
            for t in range(dp):
                part[k, t, :, cols] = both[2 * t * rows:2 * (t + 1) * rows]
            return carry

        lax.fori_loop(0, half // tile, one, 0)
        for j in range(1, nx + 1):
            d_copy(k, lax.rem(x + j, nx)).start()

    def reduce(k):
        for j in range(1, nx):
            xo = lax.rem(x + j, nx)
            d_copy(k, xo).wait_recv()
            sent[k, j - 1] = encode(part[k, 2 * xo + core] + other[k, xo], gain)
            x_copy(k, j).start()

    def pass_on(p):
        g_wait(chunk(2 * p))
        y_copy(p).start()

    def step(k, carry):
        p, h = k // 2, lax.rem(k, 2)

        @pl.when(h == 0)
        def _():
            g_wait(chunk(k + 1))

            @pl.when(jnp.logical_and(p > 0, p + 1 < nz))
            def _():
                pass_on(p + 1)

            unpack(p)

        compute(k)

        @pl.when(jnp.logical_and(k == 0, nz > 1))
        def _():
            pass_on(1)

        @pl.when(k > 0)
        def _():
            reduce(k - 1)

        return carry

    lax.fori_loop(0, mp, step, 0)
    reduce(mp - 1)

    gtotal = gsum[...]
    for j in range(1, mp):
        gb_copy(j).wait_recv()
        gtotal = gtotal + grecv_b[j]
    gblock[...] = gtotal
    gain_out[d] = gtotal

    def go_copy(j):
        return remote(gblock, gain_out.at[d], go_send.at[j], go_recv.at[j], (lax.rem(d + j, dp), m))

    for j in range(1, dp):
        go_copy(j).start()

    def finish(k, carry):
        p, h = k // 2, lax.rem(k, 2)
        d_copy(k, x).wait_recv()
        for j in range(1, nx):
            x_copy(k, j).wait_recv()
        value = part[k, d] + other[k, x]
        for j in range(1, nx):
            value = value + decode(got[k, j - 1], gain)
        cols = pl.ds(pl.multiple_of(h * half, LANES), half)
        for q in range(2):
            mc = chunk(2 * p + q)
            size = grad[mc, d][:, feat:].astype(jnp.float32)[:, :1]
            out_ref[mc, :, cols] = value[q * rows:(q + 1) * rows] * size
        return carry

    lax.fori_loop(0, mp, finish, 0)

    for j in range(1, dp):
        go_copy(j).wait()
        a_copy(j).wait_send()
        ga_copy(j).wait_send()
    for j in range(1, mp):
        gb_copy(j).wait_send()
    for p in range(nz):
        y_copy(p).wait_send()
    for p in range(1, nz):
        z_copy(p).wait_send()

    def drain(k, carry):
        for xo in range(nx):
            d_copy(k, xo).wait_send()
        for j in range(1, nx):
            x_copy(k, j).wait_send()
        return carry

    lax.fori_loop(0, mp, drain, 0)


def fused(dp, mp, cotangent, mlp_out, post_gain, down_weight):
    rows, full = cotangent.shape
    hid, feat = down_weight.shape
    nx, nz = dp // 2, mp // 2
    gain = 2.0 ** math.floor(15.8 - math.log2(full * WEIGHT_MAX))
    half = hid // 2
    tile = next(t for t in (768, 512, 256, 128) if half % t == 0)
    bf, f32 = jnp.bfloat16, jnp.float32
    dma = pltpu.SemaphoreType.DMA
    hidden, gain_grad = pl.pallas_call(
        functools.partial(kernel, dp, mp, gain, tile),
        out_shape=(jax.ShapeDtypeStruct((mp, rows, hid), f32), jax.ShapeDtypeStruct((dp, 1, feat), f32)),
        in_specs=[pl.BlockSpec(memory_space=pltpu.VMEM)] * 3 + [pl.BlockSpec(memory_space=pl.ANY)],
        out_specs=(pl.BlockSpec(memory_space=pltpu.VMEM), pl.BlockSpec(memory_space=pltpu.VMEM)),
        scratch_shapes=[
            pltpu.VMEM((hid, feat), bf),
            pltpu.VMEM((mp, dp, rows, feat + LANES), bf),
            pltpu.VMEM((dp, rows, feat + LANES), bf),
            pltpu.VMEM((4 * dp * rows, feat), bf),
            pltpu.VMEM((mp, dp, 2 * rows, half), f32),
            pltpu.VMEM((mp, nx, 2 * rows, half), f32),
            pltpu.VMEM((mp, nx - 1, 2 * rows, half), bf),
            pltpu.VMEM((mp, nx - 1, 2 * rows, half), bf),
            pltpu.VMEM((1, feat), f32),
            pltpu.VMEM((dp, 1, feat), f32),
            pltpu.VMEM((dp, 1, feat), f32),
            pltpu.VMEM((mp, 1, feat), f32),
            pltpu.VMEM((1, feat), f32),
            dma, dma((dp,)), dma((dp,)), dma((dp,)), dma((dp,)),
            dma((mp,)), dma((nz,)), dma((nz,)), dma((mp,)), dma((mp,)),
            dma((mp, nx)), dma((mp, nx)), dma((mp, nx)), dma((mp, nx)),
            dma((dp,)), dma((dp,)),
        ],
        compiler_params=pltpu.CompilerParams(
            collective_id=0, has_side_effects=True, vmem_limit_bytes=48 * 1024 * 1024
        ),
        name="norm_gather_project_reduce",
    )(cotangent, mlp_out, post_gain.reshape(1, full), down_weight)
    return hidden.reshape(mp * rows, hid), gain_grad.reshape(full)


def plain(cotangent, mlp_out, post_gain, down_weight):
    full = cotangent.shape[1]
    forward = mlp_out.astype(jnp.float32)
    upstream = cotangent.astype(jnp.float32)
    root_mean = jnp.sqrt(jnp.mean(forward * forward, axis=1, keepdims=True) + epsilon)
    normed = forward / root_mean
    gain_part = jnp.sum(upstream * normed, axis=0)
    scaled = upstream * post_gain[None, :]
    project_sum = jnp.sum(scaled * forward, axis=1, keepdims=True)
    out_grad = scaled / root_mean - forward * project_sum / (full * root_mean**3)
    hid_units = down_weight.shape[0]
    gain_grad = lax.psum(gain_part, ("dp", "mp"))
    pieces = lax.all_to_all(out_grad, "dp", split_axis=1, concat_axis=0, tiled=True)
    partial_value = jnp.dot(
        lax.all_gather(pieces, "mp", axis=0, tiled=True),
        down_weight.astype(jnp.float32).T,
        precision=lax.Precision.HIGHEST,
    )
    dp_count = lax.axis_size("dp")
    mp_count = lax.axis_size("mp")
    row_count = out_grad.shape[0]
    partial_value = partial_value.reshape(mp_count, dp_count * row_count, hid_units)
    summed = lax.psum_scatter(partial_value, "dp", scatter_dimension=1, tiled=True)
    return summed.reshape(mp_count * row_count, hid_units), gain_grad


def local(dp, mp, cotangent, mlp_out, post_gain, down_weight, gate_pre, up_pre):
    rows = cotangent.shape[0]
    hid, feat = down_weight.shape
    held_bytes = mp * rows * hid * (4 * dp + 4 * dp // 2 + 2 * dp + 4) + 2 * hid * feat
    tiled = rows % 16 == 0 and hid % (2 * LANES) == 0 and feat % LANES == 0
    paired = dp % 2 == 0 and mp % 2 == 0 and dp > 2
    if tiled and paired and held_bytes < 40 * 1024 * 1024:
        hidden_grad, gain_grad = fused(dp, mp, cotangent, mlp_out, post_gain, down_weight)
    else:
        hidden_grad, gain_grad = plain(cotangent, mlp_out, post_gain, down_weight)
    gate_val = gate_pre.astype(jnp.float32)
    up_val = up_pre.astype(jnp.float32)
    act_val, pull_back = jax.vjp(gelu_tanh, gate_val)
    gate_grad = pull_back(hidden_grad * up_val)[0]
    up_grad = hidden_grad * act_val
    return (gate_grad, up_grad, gain_grad)


def solution(mesh):
    return jax.shard_map(
        functools.partial(local, mesh.shape["dp"], mesh.shape["mp"]),
        mesh=mesh,
        in_specs=(
            P(("dp", "mp"), None),
            P(("dp", "mp"), None),
            P(),
            P("mp", "dp"),
            P("dp", "mp"),
            P("dp", "mp"),
        ),
        out_specs=(P("dp", "mp"), P("dp", "mp"), P()),
        check_vma=False,
    )
```

profile of v0, /device:TPU:1, one launch (start us, length us, event | category | flops | bytes accessed | tf_op | source)
XLA Modules:
  0.0 57.0 jit_solution(1987905368668647876)
XLA Ops:
  0.6 0.7 %reshape.15.post_ref = f32[1,4608]{1,0:T(1,128)S(1)} reshape(f32[4608]{0:T(1024)} %param.8) | data formatting | bytes 36864 | tf_op jit(solution)/shard_map/reshape | solution.py:308
  1.4 0.0 copy-start
  1.4 0.9 %copy-done = bf16[16,4608]{1,0:T(8,128)(2,1)S(1)} copy-done((bf16[16,4608]{1,0:T(8,128)(2,1)S(1)}, bf16[16,4608]{1,0:T(8,128)(2,1)}, u32[]{:S(2)}) %copy-start) | copy-done | bytes 147480
  2.3 0.0 copy-start.1
  2.3 0.9 %copy-done.1 = bf16[16,4608]{1,0:T(8,128)(2,1)S(1)} copy-done((bf16[16,4608]{1,0:T(8,128)(2,1)S(1)}, bf16[16,4608]{1,0:T(8,128)(2,1)}, u32[]{:S(2)}) %copy-start.1) | copy-done | bytes 147480
  3.2 0.0 copy-start.2
  3.2 0.0 copy-start.3
  3.2 49.0 %norm_gather_project_reduce.1 = (f32[8,16,4608]{2,1,0:T(8,128)S(1)}, f32[4,1,1152]{2,1,0:T(1,128)S(1)}) custom-call(bf16[16,4608]{1,0:T(8,128)(2,1)S(1)} %copy-done, bf16[16,4608]{1,0:T(8,128)(2,1)S(1)} %copy-done.1, f32[1,4608]{1,0:T(1,128)S(1)} %reshape.15.post_ref, bf16[4608,1152]{1,0:T(8,128)(2,1)} %w_hbm.1), custom_call_target="tpu_custom_call" | custom-call | tf_op jit(solution)/shard_map/norm_gather_project_reduce/pallas_call | solution.py:280
  52.2 0.0 copy-done.2
  52.2 0.0 copy-done.3
  52.2 4.1 %fusion.8 = (f32[128,4608]{1,0:T(8,128)}, f32[128,4608]{1,0:T(8,128)}) fusion(bf16[128,4608]{1,0:T(8,128)(2,1)S(1)} %copy-done.2, f32[8,16,4608]{2,1,0:T(8,128)S(1)} %get-tuple-element.5, bf16[128,4608]{1,0:T(8,128)(2,1)S(1)} %copy-done.3), kind=kLoop, calls=%fused_computation.13 | loop fusion | flops 14155776 | bytes 9437184 | tf_op jit(solution)/shard_map/mul | solution.py:352
  56.3 0.1 reduce
  56.3 0.6 %reshape.17 = f32[4608]{0:T(1024)} reshape(f32[4,1152]{1,0:T(4,128)S(1)} %reduce) | data formatting | bytes 36864 | tf_op jit(solution)/shard_map/reshape | solution.py:309
Async XLA Ops:
  1.4 0.9 %copy-start = (bf16[16,4608]{1,0:T(8,128)(2,1)S(1)}, bf16[16,4608]{1,0:T(8,128)(2,1)}, u32[]{:S(2)}) copy-start(bf16[16,4608]{1,0:T(8,128)(2,1)} %c_ref.1) | copy-start | bytes 442372
  2.3 0.9 %copy-start.1 = (bf16[16,4608]{1,0:T(8,128)(2,1)S(1)}, bf16[16,4608]{1,0:T(8,128)(2,1)}, u32[]{:S(2)}) copy-start(bf16[16,4608]{1,0:T(8,128)(2,1)} %y_ref.1) | copy-start | bytes 442372
  3.2 49.0 %copy-start.2 = (bf16[128,4608]{1,0:T(8,128)(2,1)S(1)}, bf16[128,4608]{1,0:T(8,128)(2,1)}, u32[]{:S(2)}) copy-start(bf16[128,4608]{1,0:T(8,128)(2,1)} %param.10) | copy-start | bytes 3538948
  3.2 49.0 %copy-start.3 = (bf16[128,4608]{1,0:T(8,128)(2,1)S(1)}, bf16[128,4608]{1,0:T(8,128)(2,1)}, u32[]{:S(2)}) copy-start(bf16[128,4608]{1,0:T(8,128)(2,1)} %param.11) | copy-start | bytes 3538948
where the time goes:
time: 57.8 us; the launch traced here: 57 us
  Pallas kernels  49 us (85%)
  other arithmetic  4.14 us (7%)
  local copies, waits for them, and re-layouts  3.18 us (6%)
  between operations  0.67 us (1%)
    pallas_call x1, Pallas kernels, fused(): pl.pallas_call(functools.partial(kernel, dp, mp, gain, tile), out_shape=(...  49 us
    mul x1, other arithmetic, local(): up_grad = hidden_grad * act_val  4.08 us
    unnamed x8, local copies, waits for them, and re-layouts  1.82 us

commit v1 on v0

v1 whole, which is shorter than its diff:
```python
import functools
import math

import jax
import jax.numpy as jnp
from jax import lax
from jax.experimental import pallas as pl
from jax.experimental.pallas import tpu as pltpu
from jax.sharding import PartitionSpec as P

MESH = pl.DeviceIdType.MESH
LANES = 128
WEIGHT_MAX = 0.09375

epsilon = 1e-06


def gelu_tanh(values):
    return jax.nn.gelu(values, approximate=True)


def encode(v):
    v2 = v * v
    v4 = v2 * v2
    return (v2 * v * v4 * jnp.abs(v)).astype(jnp.bfloat16)


def decode(codes):
    b = codes.astype(jnp.float32)
    size = jnp.abs(b)
    root = jnp.exp2(jnp.log2(size) * 0.125)
    root = jnp.where(size > 0, root, 0.0)
    return jnp.where(b < 0, -root, root)


def groups_of(mp):
    away = [(0, 1), (1, 1), (2, 1)]
    start = 3
    while start < mp:
        count = min(2, mp - start) if mp - start > 3 else mp - start
        away.append((start, count))
        start += count
    step = min(4, mp)
    home = [(q, step) for q in range(0, mp, step)]
    order = [(0, g) for g in range(len(away))] + [(1, g) for g in range(len(home))]
    return away, home, order


def kernel(
    dp, mp, gain, tile, wide,
    c_hbm, y_hbm, post_hbm, w_hbm, gate_hbm, up_hbm, gate_out, up_out, gain_out,
    c_ref, y_ref, post_ref, w_ref, wt_ref, gate_ref, up_ref,
    code, grad, size_ref, lhs, mine, dsend, drecv, xsend, got,
    gsend_a, grecv_a, gsum, grecv_b, gblock, gall,
    in_sem, w_sem, act_sem, a_send, a_recv, s_send, s_recv, ga_send, ga_recv, gb_send, gb_recv, go_send, go_recv,
    z_send, y_send, g_recv, d_send, d_recv, x_send, x_recv,
):
    d, m = lax.axis_index("dp"), lax.axis_index("mp")
    nz = mp // 2
    x, core = d // 2, lax.rem(d, 2)
    z, y = m // 2, lax.rem(m, 2)
    rows, full = c_ref.shape
    hid, feat = w_ref.shape
    tiles = hid // tile
    away, home, order = groups_of(mp)

    def remote(src, dst, send, recv, dev):
        return pltpu.make_async_remote_copy(
            src_ref=src, dst_ref=dst, send_sem=send, recv_sem=recv, device_id=dev, device_id_type=MESH
        )

    first = [
        pltpu.make_async_copy(y_hbm, y_ref, in_sem.at[0]),
        pltpu.make_async_copy(c_hbm, c_ref, in_sem.at[1]),
        pltpu.make_async_copy(post_hbm, post_ref, in_sem.at[2]),
    ]
    for copy in first:
        copy.start()

    def many(h, g):
        return 1 if (h, g) == (0, 0) else wide

    def slot(h, g):
        n = order.index((h, g))
        return sum(tiles // many(*one) for one in order[:n])

    def lag(h, g):
        return min(4, tiles) if many(h, g) == 1 else min(2, tiles // wide)

    def w_copy(i):
        units = pl.ds(pl.multiple_of(i * (wide * tile), wide * tile), wide * tile)
        return pltpu.make_async_copy(w_hbm.at[units, :], w_ref.at[units, :], w_sem.at[i])

    acts = [
        pltpu.make_async_copy(gate_hbm, gate_ref, act_sem.at[0]),
        pltpu.make_async_copy(up_hbm, up_ref, act_sem.at[1]),
    ]
    barrier = pltpu.get_barrier_semaphore()
    for j in range(1, dp):
        pl.semaphore_signal(barrier, inc=1, device_id=(lax.rem(d + j, dp), m), device_id_type=MESH)
    for j in range(1, mp):
        pl.semaphore_signal(barrier, inc=1, device_id=(d, lax.rem(m + j, mp)), device_id_type=MESH)

    for copy in first:
        copy.wait()
    for i in range(tiles // wide):
        w_copy(i).start()
    forward = y_ref[...].astype(jnp.float32)
    upstream = c_ref[...].astype(jnp.float32)
    inv = 1.0 / jnp.sqrt(jnp.mean(forward * forward, axis=1, keepdims=True) + epsilon)
    normed = forward * inv
    scaled = upstream * post_ref[...].reshape(1, full)
    mean_prod = jnp.sum(scaled * normed, axis=1, keepdims=True) * (1.0 / full)
    out_grad = (scaled - normed * mean_prod) * inv
    top = jnp.max(jnp.abs(out_grad), axis=1, keepdims=True)
    top = jnp.where(top > 1e-37, top, 1.0)
    codes = encode(out_grad * (gain / top))
    for t in range(dp):
        code[t] = codes[:, t * feat:(t + 1) * feat]
    grad[1, m, core] = code[d]
    size_ref[m] = jnp.broadcast_to(top * (1.0 / gain), (rows, LANES))

    pl.semaphore_wait(barrier, dp - 1 + mp - 1)

    def a_far(c):
        t = 2 * (1 - x) + c
        return remote(code.at[t], grad.at[0, m, core], a_send.at[c], a_recv.at[core], (t, m))

    def a_far_wait(c):
        t = 2 * (1 - x) + c
        return remote(code.at[t], grad.at[0, m, c], a_send.at[c], a_recv.at[c], (t, m))

    def a_near():
        t = 2 * x + 1 - core
        return remote(code.at[t], grad.at[1, m, core], a_send.at[2], a_recv.at[2], (t, m))

    for c in range(2):
        a_far(c).start()
    a_near().start()

    gain_part = jnp.sum(upstream * normed, axis=0, keepdims=True)
    for t in range(dp):
        gsend_a[t] = gain_part[:, t * feat:(t + 1) * feat]

    def ga_copy(j):
        t = lax.rem(d + j, dp)
        return remote(gsend_a.at[t], grecv_a.at[j], ga_send, ga_recv, (t, m))

    def ga_all():
        return remote(gsend_a.at[pl.ds(1, dp - 1)], grecv_a.at[pl.ds(1, dp - 1)], ga_send, ga_recv, (lax.rem(d + 1, dp), m))

    for j in range(1, dp):
        ga_copy(j).start()

    def turn_over(i, carry):
        units = pl.ds(pl.multiple_of(i * (wide * tile), wide * tile), wide * tile)
        w_copy(i).wait()
        wt_ref[:, units] = w_ref[units, :].T
        return carry

    lax.fori_loop(0, tiles // wide, turn_over, 0)
    for copy in acts:
        copy.start()

    def s_copy(j):
        return remote(size_ref.at[m], size_ref.at[m], s_send, s_recv, (d, lax.rem(m + j, mp)))

    def s_all():
        some = pl.ds(0, mp - 1)
        return remote(size_ref.at[some], size_ref.at[some], s_send, s_recv, (d, lax.rem(m + 1, mp)))

    def place_z(p):
        low = jnp.minimum(z, nz - 1 - z)
        odd = p % 2
        near = z + odd * ((p + 1) // 2) - (1 - odd) * (p // 2)
        up = jnp.where(2 * z < nz - 1, 1, -1)
        return jnp.where(p <= 2 * low, near, z + up * (p - low))

    def level(q):
        if q == 2:
            return 1, True
        if q == mp - 1:
            return nz - 1, False
        return ((q + 1) // 2, True) if q % 2 else ((q - 2) // 2, False)

    def place(q):
        if q == 0:
            return m
        if q == 1:
            return 2 * z + 1 - y
        p, same = level(q)
        return 2 * place_z(p) + (y if same else 1 - y)

    def z_copy(h, p):
        return remote(grad.at[h, m], grad.at[h, m], z_send, g_recv.at[h, m], (d, 2 * place_z(p) + y))

    def y_copy(h, p):
        mc = 2 * place_z(p) + y if p else m
        return remote(grad.at[h, mc], grad.at[h, mc], y_send, g_recv.at[h, mc], (d, 2 * z + 1 - y))

    def g_wait(h, q):
        mc = place(q)
        remote(grad.at[h, mc], grad.at[h, mc], y_send, g_recv.at[h, mc], (d, 2 * z + 1 - y)).wait_recv()

    def spread_z(h):
        for p in range(1, nz):
            z_copy(h, p).start()

    def d_copy(h, g, i):
        q, n = (away, home)[h][g]
        at, some = pl.ds(q * rows, n * rows), pl.ds(i * many(h, g), many(h, g))
        return remote(
            dsend.at[h, some, at, :], drecv.at[h, some, at, :], d_send, d_recv.at[slot(h, g) + i],
            (2 * x + 1 - core, m),
        )

    def x_copy(g, i):
        q, n = away[g]
        at, some = pl.ds(q * rows, n * rows), pl.ds(i * many(0, g), many(0, g))
        return remote(
            xsend.at[some, at, :], got.at[some, at, :], x_send, x_recv.at[slot(0, g) + i], (2 * (1 - x) + core, m)
        )

    def unpack(h, g):
        q0, n = (away, home)[h][g]
        base, span = 4 * q0 * rows, n * rows
        for k in range(n):
            mc = place(q0 + k)
            for s in range(2):
                value = decode(grad[h, mc, core if s == 0 else 1 - core])
                high = value.astype(jnp.bfloat16)
                at = base + s * span + k * rows
                lhs[h, at:at + rows, :] = high
                lhs[h, at + 2 * span:at + 2 * span + rows, :] = (value - high.astype(jnp.float32)).astype(jnp.bfloat16)

    def compute(h, g, i):
        q, n = (away, home)[h][g]
        base, span = 4 * q * rows, n * rows
        width = many(h, g) * tile
        units = pl.ds(pl.multiple_of(i * width, width), width)
        both = lax.dot_general(
            lhs[h, base:base + 4 * span, :], wt_ref[:, units], (((1,), (0,)), ((), ())),
            preferred_element_type=jnp.float32,
        )
        both = both[:2 * span] + both[2 * span:]
        for k in range(many(h, g)):
            cols = slice(k * tile, (k + 1) * tile)
            mine[h, i * many(h, g) + k, q * rows:q * rows + span, :] = both[:span, cols]
            dsend[h, i * many(h, g) + k, q * rows:q * rows + span, :] = both[span:, cols]
        d_copy(h, g, i).start()

    def reduce(h, g, i):
        d_copy(h, g, i).wait_recv()
        if h == 0:
            q, n = away[g]
            at = slice(q * rows, (q + n) * rows)
            for k in range(many(h, g)):
                t = i * many(h, g) + k
                xsend[t, at, :] = encode(mine[0, t, at, :] + drecv[0, t, at, :])
            x_copy(g, i).start()

    def steps(h, g):
        return tiles // many(h, g)

    def run(n):
        h, g = order[n]
        late = lag(h, g)
        left = lag(*order[n - 1]) if n > 1 else 0
        each = -(-left // steps(h, g))

        def one(i, carry):
            compute(h, g, i)
            for k in range(each):
                j = i * each + k

                @pl.when(j < left)
                def _():
                    reduce(*order[n - 1], steps(*order[n - 1]) - left + j)

            @pl.when(i >= late)
            def _():
                reduce(h, g, i - late)

            return carry

        lax.fori_loop(0, steps(h, g), one, 0)

    def flush(n):
        h, g = order[n]

        def one(i, carry):
            reduce(h, g, i)
            return carry

        lax.fori_loop(steps(h, g) - lag(h, g), steps(h, g), one, 0)

    waited = [{0}, {0}]

    def arrive(h, q):
        if q in waited[h]:
            return
        waited[h].add(q)
        g_wait(h, q)
        if q > 1 and level(q)[1]:
            y_copy(h, level(q)[0]).start()

    def ready(h, g):
        q0, n = (away, home)[h][g]
        for q in range(q0, q0 + n):
            arrive(h, q)
        unpack(h, g)

    for c in range(2):
        a_far_wait(c).wait_recv()
    y_copy(0, 0).start()
    spread_z(0)
    for j in range(1, mp):
        s_copy(j).start()

    def near_wait():
        remote(code.at[0], grad.at[1, m, 1 - core], a_send.at[2], a_recv.at[2], (2 * x + 1 - core, m)).wait_recv()

    def gb_copy(j):
        return remote(gsum, grecv_b.at[j], gb_send, gb_recv, (d, lax.rem(m + j, mp)))

    def gb_all():
        some = grecv_b.at[pl.ds(1, mp - 1)]
        return remote(some, some, gb_send, gb_recv, (d, lax.rem(m + 1, mp)))

    def go_copy(j):
        return remote(gblock, gall.at[d], go_send, go_recv, (lax.rem(d + j, dp), m))

    def go_all():
        some = gall.at[pl.ds(0, dp - 1)]
        return remote(some, some, go_send, go_recv, (lax.rem(d + 1, dp), m))

    for n in range(len(order)):
        if n == 3 or order[n] == (1, 0):
            for q in range(2, mp):
                if level(q)[1]:
                    arrive(order[n][0], q)
        ready(*order[n])
        run(n)
        if n == 0:
            flush(n)
            near_wait()
            y_copy(1, 0).start()
            ga_all().wait_recv()
            total = gsend_a[d]
            for j in range(1, dp):
                total = total + grecv_a[j]
            gsum[...] = total
            for j in range(1, mp):
                gb_copy(j).start()
        if n == 1:
            spread_z(1)
        if order[n] == (1, 0):
            gtotal = gsum[...]
            gb_all().wait()
            for j in range(1, mp):
                gtotal = gtotal + grecv_b[j]
            gblock[...] = gtotal
            gall[d] = gtotal
            for j in range(1, dp):
                go_copy(j).start()

    flush(len(order) - 1)

    s_all().wait_recv()
    for copy in acts:
        copy.wait()

    slope = math.sqrt(2.0 / math.pi)

    def finish(g):
        q0, n = away[g]

        def one(i, carry):
            x_copy(g, i).wait_recv()
            for k in range(many(0, g)):
                t = i * many(0, g) + k
                cols = pl.ds(pl.multiple_of(t * tile, tile), tile)
                for q in range(q0, q0 + n):
                    mc = place(q)
                    at = slice(q * rows, (q + 1) * rows)
                    value = mine[1, t, at, :] + drecv[1, t, at, :] + decode(got[t, at, :])
                    value = value * size_ref[mc][:, :1]
                    gate = gate_ref[mc, :, cols].astype(jnp.float32)
                    up = up_ref[mc, :, cols].astype(jnp.float32)
                    square = gate * gate
                    bent = jnp.tanh(gate * (slope + (slope * 0.044715) * square))
                    half = 0.5 + 0.5 * bent
                    up_out[mc, :, cols] = value * (gate * half)
                    turn = half + (0.5 * gate) * (1.0 - bent * bent) * (slope + (3.0 * slope * 0.044715) * square)
                    gate_out[mc, :, cols] = (value * up) * turn
            return carry

        lax.fori_loop(0, steps(0, g), one, 0)

    for g in range(len(away)):
        finish(g)

    go_all().wait()
    for t in range(dp):
        gain_out[t * feat:(t + 1) * feat] = gall[t].reshape(feat)

    a_far(0).wait_send()
    a_far(1).wait_send()
    a_near().wait_send()
    ga_all().wait_send()
    s_all().wait_send()
    remote(grad.at[0], grad.at[0], y_send, g_recv.at[0, m], (d, 2 * z + 1 - y)).wait_send()
    some = grad.at[0, pl.ds(0, 2 * (nz - 1))]
    remote(some, some, z_send, g_recv.at[0, m], (d, 2 * z + 1 - y)).wait_send()
    remote(dsend, drecv, d_send, d_recv.at[0], (2 * x + 1 - core, m)).wait_send()
    remote(xsend, got, x_send, x_recv.at[0], (2 * (1 - x) + core, m)).wait_send()


def store(gate_in, up_in, gain_in, gate_to, up_to, gain_to, sem):
    copies = [
        pltpu.make_async_copy(src, dst, sem.at[n])
        for n, (src, dst) in enumerate(((gate_in, gate_to), (up_in, up_to), (gain_in, gain_to)))
    ]
    for copy in copies:
        copy.start()
    for copy in copies:
        copy.wait()


def fused(dp, mp, cotangent, mlp_out, post_gain, down_weight, gate_pre, up_pre):
    rows, full = cotangent.shape
    hid, feat = down_weight.shape
    nz = mp // 2
    gain = 2.0 ** math.floor(15.8 - math.log2(full * WEIGHT_MAX))
    tile = tile_of(hid)
    tiles = hid // tile
    wide = next(k for k in (3, 2, 1) if tiles % k == 0)
    bf, f32 = jnp.bfloat16, jnp.float32
    dma = pltpu.SemaphoreType.DMA
    span = mp * rows
    steps = tiles + tiles // wide * (len(groups_of(mp)[2]) - 1)
    hbm_spec = pl.BlockSpec(memory_space=pltpu.HBM)
    vmem_spec = pl.BlockSpec(memory_space=pltpu.VMEM)
    gate_grad, up_grad, gain_grad = pl.pallas_call(
        functools.partial(kernel, dp, mp, gain, tile, wide),
        out_shape=(
            pltpu.VMEM((mp, rows, hid), f32),
            pltpu.VMEM((mp, rows, hid), f32),
            pltpu.VMEM((full,), f32),
        ),
        in_specs=[hbm_spec] * 6,
        out_specs=(vmem_spec,) * 3,
        scratch_shapes=[
            pltpu.VMEM((rows, full), bf),
            pltpu.VMEM((rows, full), bf),
            pltpu.VMEM((full,), f32),
            pltpu.VMEM((hid, feat), bf),
            pltpu.VMEM((feat, hid), bf),
            pltpu.VMEM((mp, rows, hid), bf),
            pltpu.VMEM((mp, rows, hid), bf),
            pltpu.VMEM((dp, rows, feat), bf),
            pltpu.VMEM((2, mp, 2, rows, feat), bf),
            pltpu.VMEM((mp, rows, LANES), f32),
            pltpu.VMEM((2, 4 * span, feat), bf),
            pltpu.VMEM((2, tiles, span, tile), f32),
            pltpu.VMEM((2, tiles, span, tile), f32),
            pltpu.VMEM((2, tiles, span, tile), f32),
            pltpu.VMEM((tiles, span, tile), bf),
            pltpu.VMEM((tiles, span, tile), bf),
            pltpu.VMEM((dp, 1, feat), f32),
            pltpu.VMEM((dp, 1, feat), f32),
            pltpu.VMEM((1, feat), f32),
            pltpu.VMEM((mp, 1, feat), f32),
            pltpu.VMEM((1, feat), f32),
            pltpu.VMEM((dp, 1, feat), f32),
            dma((3,)), dma((tiles // wide,)), dma((2,)), dma((3,)), dma((3,)), dma, dma,
            dma, dma, dma, dma, dma, dma,
            dma, dma, dma((2, mp)),
            dma, dma((steps,)), dma, dma((steps,)),
        ],
        compiler_params=pltpu.CompilerParams(
            collective_id=0, has_side_effects=True, vmem_limit_bytes=52 * 1024 * 1024
        ),
        name="norm_gather_project_reduce",
    )(*(
        pltpu.with_memory_space_constraint(value, pltpu.HBM)
        for value in (
            cotangent, mlp_out, post_gain, down_weight,
            gate_pre.reshape(mp, rows, hid), up_pre.reshape(mp, rows, hid),
        )
    ))
    outs = (gate_grad, up_grad, gain_grad)
    gate_grad, up_grad, gain_grad = pl.pallas_call(
        store,
        out_shape=tuple(pltpu.HBM(value.shape, f32) for value in outs),
        in_specs=[vmem_spec] * 3,
        out_specs=(hbm_spec,) * 3,
        scratch_shapes=[dma((3,))],
        compiler_params=pltpu.CompilerParams(vmem_limit_bytes=20 * 1024 * 1024),
        name="store",
    )(*outs)
    return gate_grad.reshape(mp * rows, hid), up_grad.reshape(mp * rows, hid), gain_grad


def plain(cotangent, mlp_out, post_gain, down_weight):
    full = cotangent.shape[1]
    forward = mlp_out.astype(jnp.float32)
    upstream = cotangent.astype(jnp.float32)
    root_mean = jnp.sqrt(jnp.mean(forward * forward, axis=1, keepdims=True) + epsilon)
    normed = forward / root_mean
    gain_part = jnp.sum(upstream * normed, axis=0)
    scaled = upstream * post_gain[None, :]
    project_sum = jnp.sum(scaled * forward, axis=1, keepdims=True)
    out_grad = scaled / root_mean - forward * project_sum / (full * root_mean**3)
    hid_units = down_weight.shape[0]
    gain_grad = lax.psum(gain_part, ("dp", "mp"))
    pieces = lax.all_to_all(out_grad, "dp", split_axis=1, concat_axis=0, tiled=True)
    partial_value = jnp.dot(
        lax.all_gather(pieces, "mp", axis=0, tiled=True),
        down_weight.astype(jnp.float32).T,
        precision=lax.Precision.HIGHEST,
    )
    dp_count = lax.axis_size("dp")
    mp_count = lax.axis_size("mp")
    row_count = out_grad.shape[0]
    partial_value = partial_value.reshape(mp_count, dp_count * row_count, hid_units)
    summed = lax.psum_scatter(partial_value, "dp", scatter_dimension=1, tiled=True)
    return summed.reshape(mp_count * row_count, hid_units), gain_grad


def tile_of(hid):
    return next((t for t in (512, 256, 128) if hid % t == 0), 0)


def local(dp, mp, cotangent, mlp_out, post_gain, down_weight, gate_pre, up_pre):
    rows = cotangent.shape[0]
    hid, feat = down_weight.shape
    span = mp * rows
    held_bytes = span * hid * (2 * 12 + 4 + 12) + 4 * hid * feat + 20 * span * feat
    tiled = rows % 16 == 0 and tile_of(hid) > 0 and feat % LANES == 0
    paired = dp == 4 and mp % 4 == 0
    if tiled and paired and held_bytes < 60 * 1024 * 1024:
        return fused(dp, mp, cotangent, mlp_out, post_gain, down_weight, gate_pre, up_pre)
    hidden_grad, gain_grad = plain(cotangent, mlp_out, post_gain, down_weight)
    gate_val = gate_pre.astype(jnp.float32)
    up_val = up_pre.astype(jnp.float32)
    act_val, pull_back = jax.vjp(gelu_tanh, gate_val)
    gate_grad = pull_back(hidden_grad * up_val)[0]
    up_grad = hidden_grad * act_val
    return (gate_grad, up_grad, gain_grad)


def solution(mesh):
    return jax.shard_map(
        functools.partial(local, mesh.shape["dp"], mesh.shape["mp"]),
        mesh=mesh,
        in_specs=(
            P(("dp", "mp"), None),
            P(("dp", "mp"), None),
            P(),
            P("mp", "dp"),
            P("dp", "mp"),
            P("dp", "mp"),
        ),
        out_specs=(P("dp", "mp"), P("dp", "mp"), P()),
        check_vma=False,
    )
```

time: 57.8 us -> 45.4 us (0.79); the launches traced: 57 us -> 45.2 us
  Pallas kernels: 49 us -> 44.6 us
  other arithmetic: 4.14 us -> 0 us
  local copies, waits for them, and re-layouts: 3.18 us -> 0 us
    pallas_call x1 -> x2, Pallas kernels: 49 us -> 44.6 us  [the longest x1 42.4 us: fused(): pl.pallas_call(functools.partial(kernel, dp, mp, gain, tile, wide), out_s...]
    mul x1 -> x0, other arithmetic: 4.08 us -> none  [local(): up_grad = hidden_grad * act_val]
    unnamed x8 -> x0, local copies, waits for them, and re-layouts: 1.82 us -> none
    reshape x2 -> x0, local copies, waits for them, and re-layouts: 1.36 us -> none  [the longest x1 0.74 us: fused(): post_gain.reshape(1, full)]
where the time goes in v1:
time: 45.4 us; the launch traced here: 45.2 us
  Pallas kernels  44.6 us (98%)
  between operations  0.64 us (1%)
    pallas_call x1, Pallas kernels, fused(): pl.pallas_call(functools.partial(kernel, dp, mp, gain, tile, wide), out_s...  42.4 us
    pallas_call x1, Pallas kernels, fused(): pl.pallas_call(store, out_shape=tuple((pltpu.HBM(value.shape, f32) for va...  2.21 us

profile of v1, /device:TPU:1, one launch (start us, length us, event | category | flops | bytes accessed | tf_op | source)
XLA Modules:
  0.0 45.2 jit_solution(16163004402879438811)
XLA Ops:
  0.6 42.4 %norm_gather_project_reduce.1 = (f32[8,16,4608]{2,1,0:T(8,128)S(1)}, f32[8,16,4608]{2,1,0:T(8,128)S(1)}, f32[4608]{0:T(1024)S(1)}) custom-call(bf16[16,4608]{1,0:T(8,128)(2,1)} %c_hbm.1, bf16[16,4608]{1,0:T(8,128)(2,1)} %y_hbm.1, f32[4608]{0:T(1024)} %post_hbm.1, bf16[4608,1152]{1,0:T(8,128)(2,1)} %w_hbm.1, bf16[8,16,4608]{2,1,0:T(8,128)(2,1)} %bitcast.4, ...), custom_call_target="tpu_custom_call" | custom-call | tf_op jit(solution)/shard_map/norm_gather_project_reduce/pallas_call | solution.py:444
  43.0 2.2 %store.1 = (f32[8,16,4608]{2,1,0:T(8,128)}, f32[8,16,4608]{2,1,0:T(8,128)}, f32[4608]{0:T(1024)}) custom-call(f32[8,16,4608]{2,1,0:T(8,128)S(1)} %get-tuple-element.9.gate_in, f32[8,16,4608]{2,1,0:T(8,128)S(1)} %get-tuple-element.10.up_in, f32[4608]{0:T(1024)S(1)} %get-tuple-element.11.gain_in), custom_call_target="tpu_custom_call" | custom-call | tf_op jit(solution)/shard_map/store/pallas_call | solution.py:493

commit v2 on v1

--- a/solution.py
+++ b/solution.py
@@ -11,6 +11,7 @@
 MESH = pl.DeviceIdType.MESH
 LANES = 128
 WEIGHT_MAX = 0.09375
+KEPT = 2
 
 epsilon = 1e-06
 
@@ -34,15 +35,11 @@
 
 
 def groups_of(mp):
-    away = [(0, 1), (1, 1), (2, 1)]
-    start = 3
-    while start < mp:
-        count = min(2, mp - start) if mp - start > 3 else mp - start
-        away.append((start, count))
-        start += count
-    step = min(4, mp)
-    home = [(q, step) for q in range(0, mp, step)]
-    order = [(0, g) for g in range(len(away))] + [(1, g) for g in range(len(home))]
+    away = [(q, 1) for q in range(4)] + [(q, 2) for q in range(4, mp, 2)]
+    home = [(0, 3), (3, mp - 3)]
+    order = [(0, g) for g in range(len(away))]
+    order.insert(len(away) - 1, (1, 0))
+    order.append((1, 1))
     return away, home, order
 
 
@@ -53,7 +50,7 @@
     code, grad, size_ref, lhs, mine, dsend, drecv, xsend, got,
     gsend_a, grecv_a, gsum, grecv_b, gblock, gall,
     in_sem, w_sem, act_sem, a_send, a_recv, s_send, s_recv, ga_send, ga_recv, gb_send, gb_recv, go_send, go_recv,
-    z_send, y_send, g_recv, d_send, d_recv, x_send, x_recv,
+    hello, z_send, y_send, g_recv, d_send, d_recv, x_send, x_recv,
 ):
     d, m = lax.axis_index("dp"), lax.axis_index("mp")
     nz = mp // 2
@@ -78,19 +75,21 @@
         copy.start()
 
     def many(h, g):
-        return 1 if (h, g) == (0, 0) else wide
+        return 1 if h == 0 and g < 2 else wide
 
     def slot(h, g):
         n = order.index((h, g))
         return sum(tiles // many(*one) for one in order[:n])
 
     def lag(h, g):
-        return min(4, tiles) if many(h, g) == 1 else min(2, tiles // wide)
+        return min(3, tiles) if many(h, g) == 1 else min(2, tiles // wide)
 
     def w_copy(i):
-        units = pl.ds(pl.multiple_of(i * (wide * tile), wide * tile), wide * tile)
+        units = pl.ds(pl.multiple_of(i * tile, tile), tile)
         return pltpu.make_async_copy(w_hbm.at[units, :], w_ref.at[units, :], w_sem.at[i])
 
+    for i in range(tiles):
+        w_copy(i).start(priority=1)
     acts = [
         pltpu.make_async_copy(gate_hbm, gate_ref, act_sem.at[0]),
         pltpu.make_async_copy(up_hbm, up_ref, act_sem.at[1]),
@@ -99,12 +98,12 @@
     for j in range(1, dp):
         pl.semaphore_signal(barrier, inc=1, device_id=(lax.rem(d + j, dp), m), device_id_type=MESH)
     for j in range(1, mp):
-        pl.semaphore_signal(barrier, inc=1, device_id=(d, lax.rem(m + j, mp)), device_id_type=MESH)
+        @pl.when(m + j < mp)
+        def _():
+            pl.semaphore_signal(barrier, inc=1, device_id=(d, m + j), device_id_type=MESH)
 
     for copy in first:
         copy.wait()
-    for i in range(tiles // wide):
-        w_copy(i).start()
     forward = y_ref[...].astype(jnp.float32)
     upstream = c_ref[...].astype(jnp.float32)
     inv = 1.0 / jnp.sqrt(jnp.mean(forward * forward, axis=1, keepdims=True) + epsilon)
@@ -120,7 +119,7 @@
     grad[1, m, core] = code[d]
     size_ref[m] = jnp.broadcast_to(top * (1.0 / gain), (rows, LANES))
 
-    pl.semaphore_wait(barrier, dp - 1 + mp - 1)
+    pl.semaphore_wait(barrier, dp - 1 + m)
 
     def a_far(c):
         t = 2 * (1 - x) + c
@@ -138,6 +137,16 @@
         a_far(c).start()
     a_near().start()
 
+    for j in range(1, mp):
+        @pl.when(m - j >= 0)
+        def _():
+            pl.semaphore_signal(hello.at[m], inc=1, device_id=(d, m - j), device_id_type=MESH)
+
+    def greet(mc):
+        @pl.when(mc > m)
+        def _():
+            pl.semaphore_wait(hello.at[mc], 1)
+
     gain_part = jnp.sum(upstream * normed, axis=0, keepdims=True)
     for t in range(dp):
         gsend_a[t] = gain_part[:, t * feat:(t + 1) * feat]
@@ -154,7 +163,8 @@
 
     def turn_over(i, carry):
         units = pl.ds(pl.multiple_of(i * (wide * tile), wide * tile), wide * tile)
-        w_copy(i).wait()
+        for k in range(wide):
+            w_copy(i * wide + k).wait()
         wt_ref[:, units] = w_ref[units, :].T
         return carry
 
@@ -172,16 +182,14 @@
     def place_z(p):
         low = jnp.minimum(z, nz - 1 - z)
         odd = p % 2
-        near = z + odd * ((p + 1) // 2) - (1 - odd) * (p // 2)
+        near = z - odd * ((p + 1) // 2) + (1 - odd) * (p // 2)
         up = jnp.where(2 * z < nz - 1, 1, -1)
         return jnp.where(p <= 2 * low, near, z + up * (p - low))
 
     def level(q):
-        if q == 2:
-            return 1, True
-        if q == mp - 1:
-            return nz - 1, False
-        return ((q + 1) // 2, True) if q % 2 else ((q - 2) // 2, False)
+        if q < 4:
+            return 1, q == 2
+        return (q - 2, True) if q < nz + 2 else (q - nz, False)
 
     def place(q):
         if q == 0:
@@ -202,9 +210,13 @@
         mc = place(q)
         remote(grad.at[h, mc], grad.at[h, mc], y_send, g_recv.at[h, mc], (d, 2 * z + 1 - y)).wait_recv()
 
-    def spread_z(h):
+    def spread_z(h, low, high):
         for p in range(1, nz):
-            z_copy(h, p).start()
+            away_by = jnp.abs(place_z(p) - z)
+
+            @pl.when(jnp.logical_and(away_by >= low, away_by <= high))
+            def _():
+                z_copy(h, p).start()
 
     def d_copy(h, g, i):
         q, n = (away, home)[h][g]
@@ -218,7 +230,7 @@
         q, n = away[g]
         at, some = pl.ds(q * rows, n * rows), pl.ds(i * many(0, g), many(0, g))
         return remote(
-            xsend.at[some, at, :], got.at[some, at, :], x_send, x_recv.at[slot(0, g) + i], (2 * (1 - x) + core, m)
+            xsend.at[some, at, :], got.at[some, at, :], x_send, x_recv.at[g if g < 3 else 3 + (g - 3) * (tiles // wide) + i], (2 * (1 - x) + core, m)
         )
 
     def unpack(h, g):
@@ -262,10 +274,12 @@
     def steps(h, g):
         return tiles // many(h, g)
 
-    def run(n):
+    last = len(away) - 1
+
+    def run(n, start=0, stop=None):
         h, g = order[n]
         late = lag(h, g)
-        left = lag(*order[n - 1]) if n > 1 else 0
+        left = KEPT if n == 1 else lag(*order[n - 1]) if 1 < n < len(order) - 1 else 0
         each = -(-left // steps(h, g))
 
         def one(i, carry):
@@ -283,39 +297,48 @@
 
             return carry
 
-        lax.fori_loop(0, steps(h, g), one, 0)
-
-    def flush(n):
+        lax.fori_loop(start, steps(h, g) if stop is None else stop, one, 0)
+
+    def flush(n, keep=0):
         h, g = order[n]
 
         def one(i, carry):
             reduce(h, g, i)
             return carry
 
-        lax.fori_loop(steps(h, g) - lag(h, g), steps(h, g), one, 0)
+        lax.fori_loop(steps(h, g) - lag(h, g), steps(h, g) - keep, one, 0)
 
     waited = [{0}, {0}]
+
+    passed = [{0}, {0}]
 
     def arrive(h, q):
         if q in waited[h]:
             return
         waited[h].add(q)
         g_wait(h, q)
-        if q > 1 and level(q)[1]:
-            y_copy(h, level(q)[0]).start()
+
+    def relay(h, p):
+        if p < nz and p not in passed[h]:
+            passed[h].add(p)
+            arrive(h, next(q for q in range(2, mp) if level(q) == (p, True)))
+            y_copy(h, p).start()
 
     def ready(h, g):
         q0, n = (away, home)[h][g]
         for q in range(q0, q0 + n):
+            if h == 0 and q > 2 and level(q)[1]:
+                relay(h, level(q)[0])
             arrive(h, q)
         unpack(h, g)
 
     for c in range(2):
         a_far_wait(c).wait_recv()
+    greet(place(1))
     y_copy(0, 0).start()
-    spread_z(0)
-    for j in range(1, mp):
-        s_copy(j).start()
+    for p in range(1, nz):
+        greet(2 * place_z(p) + y)
+    spread_z(0, 1, 1)
 
     def near_wait():
         remote(code.at[0], grad.at[1, m, 1 - core], a_send.at[2], a_recv.at[2], (2 * x + 1 - core, m)).wait_recv()
@@ -334,17 +357,53 @@
         some = gall.at[pl.ds(0, dp - 1)]
         return remote(some, some, go_send, go_recv, (lax.rem(d + 1, dp), m))
 
+    slope = math.sqrt(2.0 / math.pi)
+
+    def finish(g, i):
+        q0, n = away[g]
+        if g >= 3:
+            x_copy(g, i).wait_recv()
+        for k in range(many(0, g)):
+            t = i * many(0, g) + k
+            cols = pl.ds(pl.multiple_of(t * tile, tile), tile)
+            for q in range(q0, q0 + n):
+                mc = place(q)
+                at = slice(q * rows, (q + 1) * rows)
+                value = mine[1, t, at, :] + drecv[1, t, at, :] + decode(got[t, at, :])
+                value = value * size_ref[mc][:, :1]
+                gate = gate_ref[mc, :, cols].astype(jnp.float32)
+                up = up_ref[mc, :, cols].astype(jnp.float32)
+                square = gate * gate
+                bent = jnp.tanh(gate * (slope + (slope * 0.044715) * square))
+                half = 0.5 + 0.5 * bent
+                up_out[mc, :, cols] = value * (gate * half)
+                turn = half + (0.5 * gate) * (1.0 - bent * bent) * (slope + (3.0 * slope * 0.044715) * square)
+                gate_out[mc, :, cols] = (value * up) * turn
+
+    def finish_all(g):
+        at = pl.ds(away[g][0] * rows, away[g][1] * rows)
+        whole = got.at[:, at, :]
+        remote(whole, whole, x_send, x_recv.at[g], (2 * (1 - x) + core, m)).wait_recv()
+
+        def one(i, carry):
+            finish(g, i)
+            return carry
+
+        lax.fori_loop(0, steps(0, g), one, 0)
+
     for n in range(len(order)):
-        if n == 3 or order[n] == (1, 0):
-            for q in range(2, mp):
-                if level(q)[1]:
-                    arrive(order[n][0], q)
-        ready(*order[n])
-        run(n)
+        h, g = order[n]
+        ready(h, g)
         if n == 0:
-            flush(n)
+            run(n, 0, (tiles + 1) // 2)
+            spread_z(0, 2, 2)
+            run(n, (tiles + 1) // 2)
+            flush(n, KEPT)
             near_wait()
-            y_copy(1, 0).start()
+            for p in range(1, nz):
+                greet(2 * place_z(p) + 1 - y)
+            for j in range(1, mp):
+                s_copy(j).start()
             ga_all().wait_recv()
             total = gsend_a[d]
             for j in range(1, dp):
@@ -352,9 +411,37 @@
             gsum[...] = total
             for j in range(1, mp):
                 gb_copy(j).start()
-        if n == 1:
-            spread_z(1)
-        if order[n] == (1, 0):
+        elif n == 1:
+            spread_z(0, 3, nz)
+            relay(0, 1)
+            run(n, 0, (tiles + 1) // 2)
+            y_copy(1, 0).start()
+            run(n, (tiles + 1) // 2)
+        elif n == 2:
+            run(n)
+            spread_z(1, 1, 1)
+        elif n == 3:
+            run(n, 0, steps(h, g) - 1)
+            spread_z(1, 2, 2)
+            relay(0, 2)
+            run(n, steps(h, g) - 1)
+        elif n == 4:
+            run(n, 0, 1)
+            spread_z(1, 3, nz)
+            run(n, 1)
+        elif (h, g) == (1, 0):
+            run(n, 0, steps(h, g) - 1)
+            relay(1, 1)
+            run(n, steps(h, g) - 1)
+        elif (h, g) == (0, last):
+            run(n, 0, 1)
+            relay(1, 2)
+            run(n, 1)
+            for p in range(3, nz):
+                relay(1, p)
+        else:
+            run(n)
+        if (h, g) == (0, last):
             gtotal = gsum[...]
             gb_all().wait()
             for j in range(1, mp):
@@ -363,42 +450,30 @@
             gall[d] = gtotal
             for j in range(1, dp):
                 go_copy(j).start()
-
-    flush(len(order) - 1)
-
-    s_all().wait_recv()
-    for copy in acts:
-        copy.wait()
-
-    slope = math.sqrt(2.0 / math.pi)
-
-    def finish(g):
-        q0, n = away[g]
-
-        def one(i, carry):
-            x_copy(g, i).wait_recv()
-            for k in range(many(0, g)):
-                t = i * many(0, g) + k
-                cols = pl.ds(pl.multiple_of(t * tile, tile), tile)
-                for q in range(q0, q0 + n):
-                    mc = place(q)
-                    at = slice(q * rows, (q + 1) * rows)
-                    value = mine[1, t, at, :] + drecv[1, t, at, :] + decode(got[t, at, :])
-                    value = value * size_ref[mc][:, :1]
-                    gate = gate_ref[mc, :, cols].astype(jnp.float32)
-                    up = up_ref[mc, :, cols].astype(jnp.float32)
-                    square = gate * gate
-                    bent = jnp.tanh(gate * (slope + (slope * 0.044715) * square))
-                    half = 0.5 + 0.5 * bent
-                    up_out[mc, :, cols] = value * (gate * half)
-                    turn = half + (0.5 * gate) * (1.0 - bent * bent) * (slope + (3.0 * slope * 0.044715) * square)
-                    gate_out[mc, :, cols] = (value * up) * turn
-            return carry
-
-        lax.fori_loop(0, steps(0, g), one, 0)
-
-    for g in range(len(away)):
-        finish(g)
+            s_all().wait_recv()
+            for copy in acts:
+                copy.wait()
+            flush(n)
+            for g in range(3):
+                finish_all(g)
+
+    late = steps(1, 1) - lag(1, 1)
+
+    def end(i, carry):
+        @pl.when(i >= late)
+        def _():
+            reduce(1, 1, i)
+
+        for g in range(3, last):
+            finish(g, i)
+        return carry
+
+    def end_last(i, carry):
+        finish(last, i)
+        return carry
+
+    lax.fori_loop(0, steps(1, 1), end, 0)
+    lax.fori_loop(0, steps(1, 1), end_last, 0)
 
     go_all().wait()
     for t in range(dp):
@@ -438,7 +513,7 @@
     bf, f32 = jnp.bfloat16, jnp.float32
     dma = pltpu.SemaphoreType.DMA
     span = mp * rows
-    steps = tiles + tiles // wide * (len(groups_of(mp)[2]) - 1)
+    steps = 2 * tiles + tiles // wide * (len(groups_of(mp)[2]) - 2)
     hbm_spec = pl.BlockSpec(memory_space=pltpu.HBM)
     vmem_spec = pl.BlockSpec(memory_space=pltpu.VMEM)
     gate_grad, up_grad, gain_grad = pl.pallas_call(
@@ -473,10 +548,10 @@
             pltpu.VMEM((mp, 1, feat), f32),
             pltpu.VMEM((1, feat), f32),
             pltpu.VMEM((dp, 1, feat), f32),
-            dma((3,)), dma((tiles // wide,)), dma((2,)), dma((3,)), dma((3,)), dma, dma,
+            dma((3,)), dma((tiles,)), dma((2,)), dma((3,)), dma((3,)), dma, dma,
             dma, dma, dma, dma, dma, dma,
-            dma, dma, dma((2, mp)),
-            dma, dma((steps,)), dma, dma((steps,)),
+            pltpu.SemaphoreType.REGULAR((mp,)), dma, dma, dma((2, mp)),
+            dma, dma((steps,)), dma, dma((3 + tiles // wide * (len(groups_of(mp)[0]) - 3),)),
         ],
         compiler_params=pltpu.CompilerParams(
             collective_id=0, has_side_effects=True, vmem_limit_bytes=52 * 1024 * 1024

time: 45.4 us -> 42.6 us (0.938)
  Pallas kernels: 44.6 us -> 41.8 us
    pallas_call x1, Pallas kernels: 42.4 us -> 39.6 us  [fused(): pl.pallas_call(functools.partial(kernel, dp, mp, gain, tile, wide), out_s...]
where the time goes in v2:
time: 42.6 us; the launch traced here: 42.4 us
  Pallas kernels  41.8 us (98%)
  between operations  0.64 us (2%)
    pallas_call x1, Pallas kernels, fused(): pl.pallas_call(functools.partial(kernel, dp, mp, gain, tile, wide), out_s...  39.6 us
    pallas_call x1, Pallas kernels, fused(): pl.pallas_call(store, out_shape=tuple((pltpu.HBM(value.shape, f32) for va...  2.21 us

profile of v2, /device:TPU:1, one launch (start us, length us, event | category | flops | bytes accessed | tf_op | source)
XLA Modules:
  0.0 42.4 jit_solution(17103184105164302769)
XLA Ops:
  0.6 39.6 %norm_gather_project_reduce.1 = (f32[8,16,4608]{2,1,0:T(8,128)S(1)}, f32[8,16,4608]{2,1,0:T(8,128)S(1)}, f32[4608]{0:T(1024)S(1)}) custom-call(bf16[16,4608]{1,0:T(8,128)(2,1)} %c_hbm.1, bf16[16,4608]{1,0:T(8,128)(2,1)} %y_hbm.1, f32[4608]{0:T(1024)} %post_hbm.1, bf16[4608,1152]{1,0:T(8,128)(2,1)} %w_hbm.1, bf16[8,16,4608]{2,1,0:T(8,128)(2,1)} %bitcast.4, ...), custom_call_target="tpu_custom_call" | custom-call | tf_op jit(solution)/shard_map/norm_gather_project_reduce/pallas_call | solution.py:519
  40.2 2.2 %store.1 = (f32[8,16,4608]{2,1,0:T(8,128)}, f32[8,16,4608]{2,1,0:T(8,128)}, f32[4608]{0:T(1024)}) custom-call(f32[8,16,4608]{2,1,0:T(8,128)S(1)} %get-tuple-element.9.gate_in, f32[8,16,4608]{2,1,0:T(8,128)S(1)} %get-tuple-element.10.up_in, f32[4608]{0:T(1024)S(1)} %get-tuple-element.11.gain_in), custom_call_target="tpu_custom_call" | custom-call | tf_op jit(solution)/shard_map/store/pallas_call | solution.py:568

commit v3 on v2

--- a/solution.py
+++ b/solution.py
@@ -36,10 +36,10 @@
 
 def groups_of(mp):
     away = [(q, 1) for q in range(4)] + [(q, 2) for q in range(4, mp, 2)]
-    home = [(0, 3), (3, mp - 3)]
+    home = [(0, 3), (3, mp - 5), (mp - 2, 2)]
     order = [(0, g) for g in range(len(away))]
     order.insert(len(away) - 1, (1, 0))
-    order.append((1, 1))
+    order += [(1, 1), (1, 2)]
     return away, home, order
 
 
@@ -233,10 +233,10 @@
             xsend.at[some, at, :], got.at[some, at, :], x_send, x_recv.at[g if g < 3 else 3 + (g - 3) * (tiles // wide) + i], (2 * (1 - x) + core, m)
         )
 
-    def unpack(h, g):
+    def unpack(h, g, these):
         q0, n = (away, home)[h][g]
         base, span = 4 * q0 * rows, n * rows
-        for k in range(n):
+        for k in these:
             mc = place(q0 + k)
             for s in range(2):
                 value = decode(grad[h, mc, core if s == 0 else 1 - core])
@@ -279,8 +279,8 @@
     def run(n, start=0, stop=None):
         h, g = order[n]
         late = lag(h, g)
-        left = KEPT if n == 1 else lag(*order[n - 1]) if 1 < n < len(order) - 1 else 0
-        each = -(-left // steps(h, g))
+        left = KEPT if n == 1 else lag(*order[n - 1]) if 1 < n < len(away) + 1 else 0
+        each = -(-left // steps(h, g)) if n < 2 else min(2, left)
 
         def one(i, carry):
             compute(h, g, i)
@@ -330,7 +330,10 @@
             if h == 0 and q > 2 and level(q)[1]:
                 relay(h, level(q)[0])
             arrive(h, q)
-        unpack(h, g)
+            if h == 1:
+                unpack(h, g, [q - q0])
+        if h == 0:
+            unpack(h, g, range(n))
 
     for c in range(2):
         a_far_wait(c).wait_recv()
@@ -390,6 +393,17 @@
             return carry
 
         lax.fori_loop(0, steps(0, g), one, 0)
+
+    late = steps(1, 1) - lag(1, 1)
+
+    def end(i, carry):
+        @pl.when(i >= late)
+        def _():
+            reduce(1, 1, i)
+
+        for g in range(3, last):
+            finish(g, i)
+        return carry
 
     for n in range(len(order)):
         h, g = order[n]
@@ -436,9 +450,13 @@
         elif (h, g) == (0, last):
             run(n, 0, 1)
             relay(1, 2)
-            run(n, 1)
+            run(n, 1, 2)
             for p in range(3, nz):
                 relay(1, p)
+            run(n, 2)
+        elif (h, g) == (1, 1):
+            run(n)
+            lax.fori_loop(0, steps(1, 1), end, 0)
         else:
             run(n)
         if (h, g) == (0, last):
@@ -453,31 +471,24 @@
             s_all().wait_recv()
             for copy in acts:
                 copy.wait()
-            flush(n)
-            for g in range(3):
-                finish_all(g)
-
-    late = steps(1, 1) - lag(1, 1)
-
-    def end(i, carry):
+            flush(n, 1)
+            finish_all(0)
+            reduce(h, g, steps(h, g) - 1)
+            for k in range(1, 3):
+                finish_all(k)
+
+    def end_last(i, carry):
         @pl.when(i >= late)
         def _():
-            reduce(1, 1, i)
-
-        for g in range(3, last):
-            finish(g, i)
-        return carry
-
-    def end_last(i, carry):
+            reduce(1, 2, i)
+
         finish(last, i)
         return carry
-
-    lax.fori_loop(0, steps(1, 1), end, 0)
-    lax.fori_loop(0, steps(1, 1), end_last, 0)
 
     go_all().wait()
     for t in range(dp):
         gain_out[t * feat:(t + 1) * feat] = gall[t].reshape(feat)
+    lax.fori_loop(0, steps(1, 2), end_last, 0)
 
     a_far(0).wait_send()
     a_far(1).wait_send()
@@ -492,10 +503,12 @@
 
 
 def store(gate_in, up_in, gain_in, gate_to, up_to, gain_to, sem):
-    copies = [
-        pltpu.make_async_copy(src, dst, sem.at[n])
-        for n, (src, dst) in enumerate(((gate_in, gate_to), (up_in, up_to), (gain_in, gain_to)))
-    ]
+    pairs = [(gain_in, gain_to)]
+    half = gate_in.shape[0] // 2
+    for k in range(2):
+        some = pl.ds(k * half, half)
+        pairs += [(gate_in.at[some], gate_to.at[some]), (up_in.at[some], up_to.at[some])]
+    copies = [pltpu.make_async_copy(src, dst, sem.at[n]) for n, (src, dst) in enumerate(pairs)]
     for copy in copies:
         copy.start()
     for copy in copies:
@@ -570,7 +583,7 @@
         out_shape=tuple(pltpu.HBM(value.shape, f32) for value in outs),
         in_specs=[vmem_spec] * 3,
         out_specs=(hbm_spec,) * 3,
-        scratch_shapes=[dma((3,))],
+        scratch_shapes=[dma((5,))],
         compiler_params=pltpu.CompilerParams(vmem_limit_bytes=20 * 1024 * 1024),
         name="store",
     )(*outs)

time: 42.6 us -> 42.5 us (level)
  no operation moved by 1% of the time
where the time goes in v3:
time: 42.5 us; the launch traced here: 42.4 us
  Pallas kernels  41.8 us (98%)
  between operations  0.64 us (2%)
    pallas_call x1, Pallas kernels, fused(): pl.pallas_call(functools.partial(kernel, dp, mp, gain, tile, wide), out_s...  39.5 us
    pallas_call x1, Pallas kernels, fused(): pl.pallas_call(store, out_shape=tuple((pltpu.HBM(value.shape, f32) for va...  2.23 us

profile of v3, /device:TPU:1, one launch (start us, length us, event | category | flops | bytes accessed | tf_op | source)
XLA Modules:
  0.0 42.4 jit_solution(8525501434141837194)
XLA Ops:
  0.6 39.5 %norm_gather_project_reduce.1 = (f32[8,16,4608]{2,1,0:T(8,128)S(1)}, f32[8,16,4608]{2,1,0:T(8,128)S(1)}, f32[4608]{0:T(1024)S(1)}) custom-call(bf16[16,4608]{1,0:T(8,128)(2,1)} %c_hbm.1, bf16[16,4608]{1,0:T(8,128)(2,1)} %y_hbm.1, f32[4608]{0:T(1024)} %post_hbm.1, bf16[4608,1152]{1,0:T(8,128)(2,1)} %w_hbm.1, bf16[8,16,4608]{2,1,0:T(8,128)(2,1)} %bitcast.4, ...), custom_call_target="tpu_custom_call" | custom-call | tf_op jit(solution)/shard_map/norm_gather_project_reduce/pallas_call | solution.py:532
  40.2 2.2 %store.1 = (f32[8,16,4608]{2,1,0:T(8,128)}, f32[8,16,4608]{2,1,0:T(8,128)}, f32[4608]{0:T(1024)}) custom-call(f32[8,16,4608]{2,1,0:T(8,128)S(1)} %get-tuple-element.9.gate_in, f32[8,16,4608]{2,1,0:T(8,128)S(1)} %get-tuple-element.10.up_in, f32[4608]{0:T(1024)S(1)} %get-tuple-element.11.gain_in), custom_call_target="tpu_custom_call" | custom-call | tf_op jit(solution)/shard_map/store/pallas_call | solution.py:581
